TPU v7x, 32 devices: a whole 2x2x4 slice. The times are simulated.
32 devices in a mesh: dp: 4 (over z), row: 2 (over y), fsdp: 4 (over x, core).
Axes of the slice: x: 2, y: 2, z: 4, core: 2. Of those that a mesh axis runs over, the one named last changes fastest.
Arguments:
- x_saved: bfloat16 [2, 49152, 288], P(None, ('dp', 'row', 'fsdp'))
- dy_out: bfloat16 [2, 49152, 288], P(None, ('dp', 'row', 'fsdp'))
- w_gate: bfloat16 [288, 768], P(None, ('row', 'fsdp'))
- w_up: bfloat16 [288, 768], P(None, ('row', 'fsdp'))
- w_down: bfloat16 [768, 288], P(('row', 'fsdp'))
- g_next: float32 [32, 3, 288, 768], P(('dp', 'row', 'fsdp'))
Outputs:
- output 1: bfloat16 [2, 49152, 288], P(None, ('dp', 'row', 'fsdp'))
- output 2: float32 [3, 288, 768], P(None, None, ('row', 'fsdp'))
- output 3: float32 [32, 3, 288, 768], P(('dp', 'row', 'fsdp'))
All inputs are finite; a program needn't handle non-finite values.
Results may differ from a plain program's by a relative error of at most 0.0105422.
Values are sent between devices in bfloat16 or wider.
A program may use at most 1 GiB of HBM per device.

v0:
```python
import jax
import jax.numpy as jnp
from jax import lax
from jax.sharding import PartitionSpec as P

TOK_AXES = ("dp", "row", "fsdp")
GROUP_AXES = ("row", "fsdp")


def mlp_backward(x_flat, dy_flat, w_gate, w_up, w_down):
    pre_gate = jnp.dot(x_flat, w_gate, preferred_element_type=jnp.float32)
    pre_up = jnp.dot(x_flat, w_up, preferred_element_type=jnp.float32)
    sig_gate = jax.nn.sigmoid(pre_gate)
    act_gate = pre_gate * sig_gate
    hidden = (act_gate * pre_up).astype(jnp.bfloat16)
    d_hidden = jnp.einsum("td,fd->tf", dy_flat, w_down, preferred_element_type=jnp.float32)
    d_gate = (d_hidden * pre_up * sig_gate * (1.0 + pre_gate * (1.0 - sig_gate))).astype(jnp.bfloat16)
    d_up = (d_hidden * act_gate).astype(jnp.bfloat16)
    dx_flat = (jnp.einsum("tf,df->td", d_gate, w_gate, preferred_element_type=jnp.float32) + jnp.einsum("tf,df->td", d_up, w_up, preferred_element_type=jnp.float32)).astype(jnp.bfloat16)
    grad_layer = jnp.stack([
        jnp.einsum("td,tf->df", x_flat, d_gate, preferred_element_type=jnp.float32),
        jnp.einsum("td,tf->df", x_flat, d_up, preferred_element_type=jnp.float32),
        jnp.einsum("td,tf->df", dy_flat, hidden, preferred_element_type=jnp.float32),
    ])
    return dx_flat, grad_layer


def solution(mesh):
    def local_step(x_dev, dy_dev, gate_shard, up_shard, down_shard, g_dev):
        w_gate = lax.all_gather(gate_shard, GROUP_AXES, axis=1, tiled=True)
        w_up = lax.all_gather(up_shard, GROUP_AXES, axis=1, tiled=True)
        w_down = lax.all_gather(down_shard, GROUP_AXES, axis=0, tiled=True)
        g_shard = lax.psum_scatter(g_dev[0].astype(jnp.bfloat16), GROUP_AXES, scatter_dimension=2, tiled=True)
        grad_next = lax.psum(g_shard.astype(jnp.float32), "dp")
        micro_count, tok_dev, d_model = x_dev.shape
        dx_flat, grad_layer = mlp_backward(x_dev.reshape(micro_count * tok_dev, d_model), dy_dev.reshape(micro_count * tok_dev, d_model), w_gate, w_up, w_down)
        return dx_flat.reshape(micro_count, tok_dev, d_model), grad_next, grad_layer[None]

    in_specs = (P(None, TOK_AXES, None), P(None, TOK_AXES, None), P(None, GROUP_AXES), P(None, GROUP_AXES), P(GROUP_AXES, None), P(TOK_AXES, None, None, None))
    out_specs = (P(None, TOK_AXES, None), P(None, None, GROUP_AXES), P(TOK_AXES, None, None, None))
    return jax.shard_map(local_step, mesh=mesh, in_specs=in_specs, out_specs=out_specs, check_vma=False)
```

profile of v0, /device:TPU:0, one launch (start us, length us, event | category | flops | bytes accessed | tf_op | source)
XLA Modules:
  0.0 126.1 jit_solution(14245371869222314147)
XLA Ops:
  7.2 0.0 reduce-scatter.4.cloned.1.call-start
  7.2 2.9 %convert_bitcast_fusion = bf16[3,288,768]{2,1,0:T(8,128)(2,1)} fusion(f32[1,3,288,768]{3,2,1,0:T(8,128)} %param.11), kind=kLoop, calls=%fused_computation.10 | loop fusion | flops 663552 | bytes 3981312 | tf_op jit(solution)/shard_map/convert_element_type | solution.py:33
  10.2 3.9 %copy.18 = bf16[3,288,768]{1,0,2:T(4,128)(2,1)S(1)} copy(bf16[3,288,768]{2,1,0:T(8,128)(2,1)} %convert_bitcast_fusion) | data formatting | bytes 2654208
  14.0 0.0 copy-start.3
  14.0 0.0 copy-start.4
  14.1 2.5 %reshape.19 = bf16[768,864]{1,0:T(8,128)(2,1)} reshape(bf16[768,3,288]{2,1,0:T(4,128)(2,1)S(1)} %bitcast.46) | data formatting | bytes 2654208
  16.6 0.0 reduce-scatter.4.cloned.1.call-update
  16.6 1.7 %copy.22 = bf16[2,36,8,1536]{3,2,0,1:T(8,128)(2,1)S(1)} copy(bf16[2,36,8,1536]{3,2,1,0:T(8,128)(2,1)} %bitcast.47) | data formatting | bytes 3538944 | tf_op jit(solution)/shard_map/reshape | solution.py:36
  18.3 0.0 copy-done.3
  18.3 0.1 copy.15
  18.4 11.5 %all_gather.10 = bf16[288,768]{0,1:T(8,128)(2,1)S(1)} all-gather(bf16[288,96]{0,1:T(8,128)(2,1)S(1)} %copy.15), channel_id=1, replica_groups=mesh['dp'=4,'row'=2,'fsdp'=4] {'row','fsdp'}, dimensions={1}, use_global_device_ids=true | all-gather | bytes 497664 | tf_op jit(solution)/shard_map/all_gather | solution.py:31
  29.9 0.0 copy-done.4
  29.9 0.1 copy.16
  30.1 10.0 %all_gather.11 = bf16[288,768]{0,1:T(8,128)(2,1)S(1)} all-gather(bf16[288,96]{0,1:T(8,128)(2,1)S(1)} %copy.16), channel_id=1, replica_groups=mesh['dp'=4,'row'=2,'fsdp'=4] {'row','fsdp'}, dimensions={1}, use_global_device_ids=true | all-gather | bytes 497664 | tf_op jit(solution)/shard_map/all_gather | solution.py:30
  40.0 2.7 %fusion.6 = f32[3072,768]{1,0:T(8,128)S(1)} fusion(bf16[3072,288]{0,1:T(8,128)(2,1)S(1)} %bitcast.41, bf16[288,768]{0,1:T(8,128)(2,1)S(1)} %all_gather.10), kind=kOutput, calls=%fused_computation.15 | convolution fusion | flops 1358954496 | bytes 11649024 | tf_op jit(solution)/shard_map/dot_general | solution.py:12
  42.7 0.0 copy-start.1
  42.7 0.0 copy-start.5
  42.7 5.1 %fusion.7 = f32[3072,768]{1,0:T(8,128)} fusion(bf16[3072,288]{0,1:T(8,128)(2,1)S(1)} %bitcast.42, bf16[288,768]{0,1:T(8,128)(2,1)S(1)} %all_gather.11), kind=kOutput, calls=%fused_computation.16 | convolution fusion | flops 1358954496 | bytes 11649024 | tf_op jit(solution)/shard_map/dot_general | solution.py:11
  47.8 0.0 copy-done.1
  47.8 1.4 %copy.21 = bf16[2,36,8,1536]{3,2,0,1:T(8,128)(2,1)} copy(bf16[2,36,8,1536]{3,2,1,0:T(8,128)(2,1)S(1)} %bitcast.48) | data formatting | bytes 3538944 | tf_op jit(solution)/shard_map/reshape | solution.py:36
  49.3 0.0 copy-done.5
  49.3 10.0 %all_gather.9 = bf16[768,288]{1,0:T(8,128)(2,1)S(1)} all-gather(bf16[96,288]{1,0:T(8,128)(2,1)S(1)} %copy-done.5), channel_id=1, replica_groups=mesh['dp'=4,'row'=2,'fsdp'=4] {'row','fsdp'}, dimensions={0}, use_global_device_ids=true | all-gather | bytes 497664 | tf_op jit(solution)/shard_map/all_gather | solution.py:32
  59.3 11.2 %multiply_convert_fusion.1 = (bf16[3072,768]{1,0:T(8,128)(2,1)S(1)}, bf16[3072,768]{1,0:T(8,128)(2,1)}) fusion(f32[3072,768]{1,0:T(8,128)} %fusion.7, f32[3072,768]{1,0:T(8,128)S(1)} %fusion.6, bf16[3072,288]{0,1:T(8,128)(2,1)} %bitcast.50, bf16[768,288]{1,0:T(8,128)(2,1)S(1)} %all_gather.9), kind=kOutput, calls=%fused_computation.1 | convolution fusion | flops 1389625344 | bytes 30523392 | tf_op jit(solution)/shard_map/td,fd->tf/dot_general | solution.py:16
  70.5 0.0 copy-start
  70.5 4.0 %convolution_bitcast_fusion.1 = f32[1,288,768]{2,1,0:T(8,128)S(1)} fusion(bf16[3072,288]{0,1:T(8,128)(2,1)S(1)} %bitcast.43, bf16[3072,768]{1,0:T(8,128)(2,1)} %get-tuple-element.13), kind=kOutput, calls=%fused_computation.13 | convolution fusion | flops 1358954496 | bytes 7372800 | tf_op jit(solution)/shard_map/td,tf->df/dot_general | solution.py:21
  74.5 0.0 copy-done
  74.5 1.7 %fusion.8 = f32[3072,288]{0,1:T(8,128)S(1)} fusion(bf16[3072,768]{1,0:T(8,128)(2,1)S(1)} %copy-done, bf16[288,768]{0,1:T(8,128)(2,1)S(1)} %all_gather.11), kind=kOutput, calls=%fused_computation.17 | convolution fusion | flops 1358954496 | bytes 8699904 | tf_op jit(solution)/shard_map/tf,df->td/dot_general | solution.py:19
  76.2 1.6 %convolution_bitcast_fusion = f32[1,288,768]{2,1,0:T(8,128)S(1)} fusion(bf16[3072,288]{0,1:T(8,128)(2,1)S(1)} %bitcast.44, bf16[3072,768]{1,0:T(8,128)(2,1)S(1)} %get-tuple-element.12), kind=kOutput, calls=%fused_computation.12 | convolution fusion | flops 1358954496 | bytes 7372800 | tf_op jit(solution)/shard_map/td,tf->df/dot_general | solution.py:22
  77.8 0.0 copy-start.2
  77.8 1.8 %fusion.2 = bf16[3072,288]{0,1:T(8,128)(2,1)S(1)} fusion(f32[3072,288]{0,1:T(8,128)S(1)} %fusion.8, bf16[3072,768]{1,0:T(8,128)(2,1)S(1)} %get-tuple-element.12, bf16[288,768]{0,1:T(8,128)(2,1)S(1)} %all_gather.10), kind=kOutput, calls=%fused_computation.7 | convolution fusion | flops 1360723968 | bytes 10469376 | tf_op jit(solution)/shard_map/tf,df->td/dot_general | solution.py:19
  79.6 1.3 %copy.24 = bf16[36,2,8,1536]{3,2,0,1:T(8,128)(2,1)} copy(bf16[36,2,8,1536]{3,2,1,0:T(8,128)(2,1)S(1)} %bitcast.45) | data formatting | bytes 3538944 | tf_op jit(solution)/shard_map/reshape | solution.py:37
  81.0 0.0 copy-done.2
  81.0 5.9 %fusion.4 = f32[1,288,768]{2,1,0:T(8,128)S(1)} fusion(bf16[3072,288]{0,1:T(8,128)(2,1)S(1)} %bitcast.51, f32[3072,768]{1,0:T(8,128)S(1)} %fusion.6, f32[3072,768]{1,0:T(8,128)} %fusion.7), kind=kOutput, calls=%fused_computation.11 | convolution fusion | flops 1373110272 | bytes 21528576 | tf_op jit(solution)/shard_map/td,tf->df/dot_general | solution.py:23
  86.8 1.7 %maximum_bitcast_fusion = f32[1,3,288,768]{3,2,1,0:T(8,128)} fusion(f32[1,288,768]{2,1,0:T(8,128)S(1)} %fusion.4, f32[1,288,768]{2,1,0:T(8,128)S(1)} %convolution_bitcast_fusion, f32[1,288,768]{2,1,0:T(8,128)S(1)} %convolution_bitcast_fusion.1), kind=kLoop, calls=%fused_computation.8 | loop fusion | flops 1327104 | bytes 5308416 | tf_op jit(solution)/shard_map/broadcast_in_dim | solution.py:37
  88.5 0.0 reduce-scatter.4.cloned.1.call-done
  88.5 1.1 reshape.20
  89.7 0.2 copy.19
  89.9 29.3 %all-reduce.1 = f32[3,288,96]{2,1,0:T(8,128)} all-reduce(bf16[3,288,96]{2,1,0:T(8,128)(2,1)S(1)} %copy.19), channel_id=1, replica_groups=mesh['dp'=4,'row'=2,'fsdp'=4] {'dp'}, use_global_device_ids=true, to_apply=%region_1.0 | all-reduce | flops 82944 | bytes 497664 | tf_op jit(solution)/shard_map/psum | solution.py:34
Async XLA Ops:
  7.2 81.3 %reduce-scatter.4.cloned.1.call-start = ((), (), s32[]{:S(2)}) async-start(), calls=%async_computation.1 | async-start | bytes 1548288
  14.0 4.3 %copy-start.3 = (bf16[288,96]{1,0:T(8,128)(2,1)S(1)}, bf16[288,96]{1,0:T(8,128)(2,1)}, u32[]{:S(2)}) copy-start(bf16[288,96]{1,0:T(8,128)(2,1)} %param.9) | copy-start | bytes 165892
  14.0 15.9 %copy-start.4 = (bf16[288,96]{1,0:T(8,128)(2,1)S(1)}, bf16[288,96]{1,0:T(8,128)(2,1)}, u32[]{:S(2)}) copy-start(bf16[288,96]{1,0:T(8,128)(2,1)} %param.8) | copy-start | bytes 165892
  42.7 5.1 %copy-start.1 = (bf16[2,1536,288]{1,2,0:T(8,128)(2,1)S(1)}, bf16[2,1536,288]{1,2,0:T(8,128)(2,1)}, u32[]{:S(2)}) copy-start(bf16[2,1536,288]{1,2,0:T(8,128)(2,1)} %param.7) | copy-start | bytes 5308420
  42.7 6.5 %copy-start.5 = (bf16[96,288]{1,0:T(8,128)(2,1)S(1)}, bf16[96,288]{1,0:T(8,128)(2,1)}, u32[]{:S(2)}) copy-start(bf16[96,288]{1,0:T(8,128)(2,1)} %param.10) | copy-start | bytes 165892
  70.5 4.0 %copy-start = (bf16[3072,768]{1,0:T(8,128)(2,1)S(1)}, bf16[3072,768]{1,0:T(8,128)(2,1)}, u32[]{:S(2)}) copy-start(bf16[3072,768]{1,0:T(8,128)(2,1)} %get-tuple-element.13) | copy-start | bytes 14155780
  77.8 3.1 %copy-start.2 = (bf16[2,36,8,1536]{3,2,0,1:T(8,128)(2,1)S(1)}, bf16[2,36,8,1536]{3,2,0,1:T(8,128)(2,1)}, u32[]{:S(2)}) copy-start(bf16[2,36,8,1536]{3,2,0,1:T(8,128)(2,1)} %copy.21) | copy-start | bytes 5308420
Sparse Core Ops, SparseCore 0:
  16.7 40.5 reduce-scatter.3
where the time goes:
time: 126 us
  blocking collectives  60.9 us (48%)
  matrix products  33.9 us (27%)
  between operations  14.2 us (11%)
  local copies, waits for them, and re-layouts  12.5 us (10%)
  other arithmetic  4.62 us (4%)
    psum x1, blocking collectives, local_step(): grad_next = lax.psum(g_shard.astype(jnp.float32), 'dp')  29.3 us
    all_gather x1, blocking collectives, local_step(): w_up = lax.all_gather(up_shard, GROUP_AXES, axis=1, tiled=True)  11.5 us
    dot_general x1, matrix products, mlp_backward(): jnp.einsum('td,fd->tf', dy_flat, w_down, preferred_element_type=jnp.float32)  11.2 us
    all_gather x1, blocking collectives, local_step(): w_down = lax.all_gather(down_shard, GROUP_AXES, axis=0, tiled=True)  10 us
    all_gather x1, blocking collectives, local_step(): w_gate = lax.all_gather(gate_shard, GROUP_AXES, axis=1, tiled=True)  9.99 us
    unnamed x18, local copies, waits for them, and re-layouts  8.01 us
    dot_general x1, matrix products, mlp_backward(): jnp.einsum('td,tf->df', dy_flat, hidden, preferred_element_type=jnp.float32)  5.86 us
    dot_general x1, matrix products, mlp_backward(): pre_gate = jnp.dot(x_flat, w_gate, preferred_element_type=jnp.float32)  5.08 us
  transfers between devices with their start and end apart: 1, of which 0 were waited for; matrix products, arithmetic and copies ran while one was open for 32% of the time, Pallas kernels for 0%

commit v1 on v0

v1 whole, which is shorter than its diff:
```python
import functools
import jax
import jax.numpy as jnp
from jax import lax
from jax.experimental import pallas as pl
from jax.experimental.pallas import tpu as pltpu
from jax.sharding import PartitionSpec as P

TOK_AXES = ("dp", "row", "fsdp")
GROUP_AXES = ("row", "fsdp")
MESH = pl.DeviceIdType.MESH
BF = jnp.bfloat16
F32 = jnp.float32

D = 288
FF = 768
SH = 96
LW = 896
FC = 256
TT = 512
MTOK = 1536
PIECES = ((0, 256), (256, 512), (512, 896))
NT_DIMS = (((1,), (1,)), ((), ()))
CUTS = (
    (0, 0, 0, 0, 96), (0, 96, 1, 0, 96), (0, 192, 2, 0, 64),
    (1, 0, 2, 64, 32), (1, 32, 3, 0, 96), (1, 128, 4, 0, 96), (1, 224, 5, 0, 32),
    (2, 0, 5, 32, 64), (2, 64, 6, 0, 96), (2, 160, 7, 0, 96),
)


def dot(a, b):
    return jnp.dot(a, b, preferred_element_type=F32)


def dot_nt(a, b):
    return lax.dot_general(a, b, NT_DIMS, preferred_element_type=F32)


def eye(n):
    r = lax.broadcasted_iota(jnp.int32, (n, n), 0)
    c = lax.broadcasted_iota(jnp.int32, (n, n), 1)
    return (r == c).astype(F32).astype(BF)


def body(x_hbm, dy_hbm, wg_hbm, wu_hbm, wd_hbm, g_hbm,
         dx_hbm, gn_ref, dw_hbm,
         xt, yt, wg, wu, wd, g32, wire, xtail, wn, hh, dxacc, dxo, dwa,
         gt, gr, s1, r1, s2, r2, zb,
         in_sem, out_sem, ws_sem, wrd_sem, wrp_sem, gs_sem, gr_sem, zs_sem, zr_sem):
    z = lax.axis_index("dp")
    y = lax.axis_index("row")
    f = lax.axis_index("fsdp")
    x = f // 2
    c = f % 2
    partner = (z, y, f + 1 - 2 * c)
    nbr_a = (z, y + (1 - c) * (1 - 2 * y), (f + 2 * c) % 4)
    nbr_b = (z, y + c * (1 - 2 * y), (f + 2 * (1 - c)) % 4)
    ax_a = 1 - c
    ax_b = c

    loads = [
        pltpu.make_async_copy(wg_hbm, wg, in_sem.at[0]),
        pltpu.make_async_copy(wu_hbm, wu, in_sem.at[1]),
        pltpu.make_async_copy(wd_hbm, wd, in_sem.at[2]),
        pltpu.make_async_copy(g_hbm.at[0, 0], g32.at[0], in_sem.at[3]),
        pltpu.make_async_copy(g_hbm.at[0, 1], g32.at[1], in_sem.at[4]),
        pltpu.make_async_copy(g_hbm.at[0, 2], g32.at[2], in_sem.at[5]),
        pltpu.make_async_copy(x_hbm, xt, in_sem.at[6]),
        pltpu.make_async_copy(dy_hbm, yt, in_sem.at[7]),
    ]
    for l in loads:
        l.start()

    bar = pltpu.get_barrier_semaphore()
    for dev in (partner, nbr_a, nbr_b):
        pl.semaphore_signal(bar, inc=1, device_id=dev, device_id_type=MESH)

    @pl.when(z > 0)
    def _():
        pl.semaphore_signal(bar, inc=1, device_id=(z - 1, y, f), device_id_type=MESH)

    @pl.when(z < 3)
    def _():
        pl.semaphore_signal(bar, inc=1, device_id=(z + 1, y, f), device_id_type=MESH)

    def rows_of(yy, xx, cc):
        return pl.ds(pl.multiple_of((4 * yy + 2 * xx + cc) * SH, 32), SH)

    own = rows_of(y, x, c)
    i96 = eye(SH)
    for l in loads[:3]:
        l.wait()
    wire[own, 0:256] = dot_nt(i96, wg[0:256, :]).astype(BF)
    wire[own, 256:512] = dot_nt(i96, wu[0:256, :]).astype(BF)
    wire[own, 512:768] = wd[:, 0:256]
    tails = dot_nt(i96, jnp.concatenate([wg[256:288, :], wu[256:288, :]], 0)).astype(BF)
    wire[own, 768:896] = jnp.concatenate([tails, wd[:, 256:288], jnp.zeros((SH, 32), BF)], 1)

    @pl.when(jnp.logical_and(z > 0, z < 3))
    def _():
        pl.semaphore_wait(bar, 5)

    @pl.when(jnp.logical_or(z == 0, z == 3))
    def _():
        pl.semaphore_wait(bar, 4)

    def wcopy(rows, send, recv, dev):
        return pltpu.make_async_remote_copy(
            src_ref=wire.at[rows], dst_ref=wire.at[rows], send_sem=ws_sem.at[send], recv_sem=recv,
            device_id=dev, device_id_type=MESH)

    rows_x = rows_of(y, 1 - x, c)
    rows_y = rows_of(1 - y, x, c)
    rows_d = rows_of(1 - y, 1 - x, c)
    ya = y + ax_a * (1 - 2 * y)
    xa = x + ax_b * (1 - 2 * x)
    yb = y + ax_b * (1 - 2 * y)
    xb = x + ax_a * (1 - 2 * x)
    rows_a = rows_of(ya, xa, c)
    rows_b = rows_of(yb, xb, c)
    w_own_a = wcopy(own, 0, wrd_sem.at[ax_a], nbr_a)
    w_own_b = wcopy(own, 1, wrd_sem.at[ax_b], nbr_b)
    w_own_p = wcopy(own, 2, wrp_sem.at[0], partner)
    w_fa_p = wcopy(rows_a, 3, wrp_sem.at[1 + ax_a], partner)
    w_fa_b = wcopy(rows_a, 4, wrd_sem.at[2], nbr_b)
    w_fb_p = wcopy(rows_b, 5, wrp_sem.at[1 + ax_b], partner)
    w_fd_p = wcopy(rows_d, 6, wrp_sem.at[3], partner)

    def wrecv(rows, sem):
        wcopy(rows, 0, sem, partner).wait_recv()

    w_own_a.start()
    w_own_b.start()
    w_own_p.start()

    i256 = eye(256)
    for s in range(3):
        loads[3 + s].wait()
        for fb in range(3):
            t = dot_nt(i256, g32[s, 0:256, 256 * fb:256 * fb + 256].astype(BF)).astype(BF)
            for blk, r0, sh, r, n in CUTS:
                if blk == fb:
                    gt[sh // 2, sh % 2, r:r + n, 256 * s:256 * s + 256] = t[r0:r0 + n]
        if s == 2:
            for fb in range(3):
                tl = jnp.concatenate([g32[k, 256:288, 256 * fb:256 * fb + 256].astype(BF) for k in range(3)]
                                     + [jnp.zeros((32, 256), BF)], 0)
                t = dot_nt(i256, tl).astype(BF)
                for blk, r0, sh, r, n in CUTS:
                    if blk == fb:
                        gt[sh // 2, sh % 2, r:r + n, 768:896] = t[r0:r0 + n]
        g_pair(gt, gr, gs_sem, gr_sem, s, c, partner).start()

    loads[6].wait()
    loads[7].wait()
    for m in range(2):
        sl = slice(m * MTOK, (m + 1) * MTOK)
        xtl = xt[m, 256:288]
        xtail[0, :, sl] = jnp.concatenate([xtl, jnp.zeros((96, MTOK), BF)], 0)
        xtail[1, :, sl] = jnp.concatenate([jnp.zeros((32, MTOK), BF), xtl, jnp.zeros((64, MTOK), BF)], 0)
        xtail[2, :, sl] = jnp.concatenate([jnp.zeros((64, MTOK), BF), yt[m, 256:288], jnp.zeros((32, MTOK), BF)], 0)

    def chip(ra, rb):
        ya_ = y + (1 - 2 * y) * (ra * ax_a + rb * ax_b)
        xa_ = x + (1 - 2 * x) * (ra * ax_b + rb * ax_a)
        return 2 * ya_ + xa_

    def add(p, q):
        return (p.astype(F32) + q.astype(F32)).astype(BF)

    def remote(src, dst, ssem, rsem, dev):
        return pltpu.make_async_remote_copy(src_ref=src, dst_ref=dst, send_sem=ssem, recv_sem=rsem,
                                            device_id=dev, device_id_type=MESH)

    def ph1(p):
        lo, hi = PIECES[p]
        return remote(s1.at[1, :, :, lo:hi], r1.at[:, :, lo:hi], gs_sem.at[3 + p], gr_sem.at[3 + p], nbr_a)

    def ph2(p):
        lo, hi = PIECES[p]
        return remote(s2.at[1, :, lo:hi], r2.at[:, lo:hi], gs_sem.at[6 + p], gr_sem.at[6 + p], nbr_b)

    def zcopy(slot, p, send, dz):
        lo, hi = PIECES[p]
        return remote(zb.at[slot, :, lo:hi], zb.at[slot, :, lo:hi], zs_sem.at[send, p], zr_sem.at[slot, p], (z + dz, y, f))

    def ev_pair(p):
        lo, hi = PIECES[p]
        g_pair(gt, gr, gs_sem, gr_sem, p, c, partner).wait_recv()
        for ra in (1, 0):
            for rb in range(2):
                q = chip(ra, rb)
                s1[ra, rb, :, lo:hi] = add(gt[q, c, :, lo:hi], gr[q, :, lo:hi])
        ph1(p).start()

    def ev_ph1(p):
        lo, hi = PIECES[p]
        ph1(p).wait_recv()
        for rb in (1, 0):
            s2[rb, :, lo:hi] = add(s1[0, rb, :, lo:hi], r1[rb, :, lo:hi])
        ph2(p).start()

    def ev_ph2(p):
        lo, hi = PIECES[p]
        ph2(p).wait_recv()
        zb[z, :, lo:hi] = add(s2[0, :, lo:hi], r2[:, lo:hi])

        @pl.when(z < 3)
        def _():
            zcopy(z, p, 0, 1).start()

        @pl.when(z > 0)
        def _():
            zcopy(z, p, 1, -1).start()

    def ev_z(h, p):
        @pl.when(z >= h)
        def _():
            zcopy(z - h, p, 0, 0 if False else 1).wait_recv()
            if h < 3:
                @pl.when(z < 3)
                def _():
                    zcopy(z - h, p, 2 * h, 1).start()

        @pl.when(z + h <= 3)
        def _():
            zcopy(z + h, p, 0, 1).wait_recv()
            if h < 3:
                @pl.when(z > 0)
                def _():
                    zcopy(z + h, p, 2 * h + 1, -1).start()

    def ev_final():
        t = zb[0].astype(F32) + zb[1].astype(F32) + zb[2].astype(F32) + zb[3].astype(F32)
        t = jnp.concatenate([t, jnp.zeros((32, LW), F32)], 0).T
        for s in range(3):
            gn_ref[s, 0:256, :] = t[256 * s:256 * s + 256, 0:SH]
            gn_ref[s, 256:288, :] = t[768 + 32 * s:800 + 32 * s, 0:SH]

    for p in range(3):
        ev_pair(p)
    wrecv(rows_b, wrd_sem.at[ax_b])
    w_fb_p.start()
    wrecv(rows_a, wrd_sem.at[ax_a])
    w_fa_b.start()
    w_fa_p.start()
    wrecv(rows_of(y, x, 1 - c), wrp_sem.at[0])
    wrecv(rows_of(y, 1 - x, 1 - c), wrp_sem.at[1])

    def ev_diag():
        wrecv(rows_d, wrd_sem.at[2])
        w_fd_p.start()

    def ev_rest():
        wrecv(rows_of(1 - y, x, 1 - c), wrp_sem.at[2])
        wrecv(rows_of(1 - y, 1 - x, 1 - c), wrp_sem.at[3])

    nt = 2 * MTOK // TT
    per = MTOK // TT

    events = {}

    def at(step, fn, *args):
        events.setdefault(step, []).append((fn, args))

    at(2, ev_diag)
    for p in range(3):
        at(1 + p, ev_ph1, p)
        at(3 + p, ev_ph2, p)
        at(6 + p, ev_z, 1, p)
        at(9 + p, ev_z, 2, p)
        at(12 + p, ev_z, 3, p)
    at(15, ev_final)
    at(nt, ev_rest)

    def step(it, carry):
        for k, evs in sorted(events.items()):
            @pl.when(it == k)
            def _():
                for fn, args in evs:
                    fn(*args)
        j = it // nt
        i = it % nt
        ch = j + y * (2 - 2 * j)
        rows = pl.ds(pl.multiple_of(ch * FC, FC), FC)

        @pl.when(i == 0)
        def _():
            e = eye(FC)
            t = dot_nt(e[:128, :128], wire[rows, 768:896]).astype(BF)
            for k in range(2):
                wn[k, 0:256, :] = dot_nt(e, wire[rows, 256 * k:256 * k + 256]).astype(BF)
                wn[k, 256:288, :] = t[32 * k:32 * k + 32]

        m = i // per
        col = pl.ds(pl.multiple_of((i % per) * TT, TT), TT)
        gcol = pl.ds(pl.multiple_of(i * TT, TT), TT)
        tl = wire[rows, 768:896]
        a = dot(wire[rows, 0:256], xt[m, 0:256, col]) + dot(tl, xtail[0, :, gcol])
        b = dot(wire[rows, 256:512], xt[m, 0:256, col]) + dot(tl, xtail[1, :, gcol])
        dh = dot(wire[rows, 512:768], yt[m, 0:256, col]) + dot(tl, xtail[2, :, gcol])
        s = 1.0 / (1.0 + jnp.exp(-a))
        act = a * s
        hh[0] = (dh * b * (s + act * (1.0 - s))).astype(BF)
        hh[1] = (dh * act).astype(BF)
        hh[2] = (act * b).astype(BF)
        d = dot(wn[0], hh[0]) + dot(wn[1], hh[1])

        @pl.when(j == 0)
        def _():
            dxacc[m, :, col] = d

        @pl.when(j == 1)
        def _():
            dxacc[m, :, col] = d + dxacc[m, :, col]

        @pl.when(j == 2)
        def _():
            dxo[m, :, col] = (d + dxacc[m, :, col]).astype(BF)
        for k in range(3):
            o = dot_nt(xt[m, :, col] if k < 2 else yt[m, :, col], hh[k])
            dwa[k, :, rows] = jnp.where(i == 0, o, o + dwa[k, :, rows])

        @pl.when(i == nt - 1)
        def _():
            out_dw(j, rows).start()

        @pl.when(jnp.logical_and(j == 2, i % per == per - 1))
        def _():
            pltpu.make_async_copy(dxo.at[m], dx_hbm.at[m], out_sem.at[3 + m]).start()
        return carry

    def out_dw(j, rows):
        return pltpu.make_async_copy(dwa.at[:, :, rows], dw_hbm.at[0, :, :, rows], out_sem.at[j])

    lax.fori_loop(0, 3 * nt, step, 0)

    for j in range(3):
        ch = j + y * (2 - 2 * j)
        out_dw(j, pl.ds(pl.multiple_of(ch * FC, FC), FC)).wait()
    for m in range(2):
        pltpu.make_async_copy(dxo.at[m], dx_hbm.at[m], out_sem.at[3 + m]).wait()
    for cp in (w_own_a, w_own_b, w_own_p, w_fa_p, w_fa_b, w_fb_p, w_fd_p):
        cp.wait_send()
    for p in range(3):
        g_pair(gt, gr, gs_sem, gr_sem, p, c, partner).wait_send()
        ph1(p).wait_send()
        ph2(p).wait_send()

        @pl.when(z < 3)
        def _():
            zcopy(z, p, 0, 1).wait_send()

        @pl.when(z > 0)
        def _():
            zcopy(z, p, 1, -1).wait_send()
        for h in (1, 2):
            @pl.when(jnp.logical_and(z >= h, z < 3))
            def _():
                zcopy(z - h, p, 2 * h, 1).wait_send()

            @pl.when(jnp.logical_and(z + h <= 3, z > 0))
            def _():
                zcopy(z + h, p, 2 * h + 1, -1).wait_send()


def g_pair(gt, gr, gs_sem, gr_sem, p, c, partner):
    lo, hi = PIECES[p]
    return pltpu.make_async_remote_copy(
        src_ref=gt.at[:, 1 - c, :, lo:hi], dst_ref=gr.at[:, :, lo:hi], send_sem=gs_sem.at[p], recv_sem=gr_sem.at[p],
        device_id=partner, device_id_type=MESH)


def fused(x_t, dy_t, wg, wu, wd, g):
    any_ = pl.BlockSpec(memory_space=pl.ANY)
    vm = pl.BlockSpec(memory_space=pltpu.VMEM)
    dma = pltpu.SemaphoreType.DMA
    return pl.pallas_call(
        body,
        name="mlp_bwd",
        out_shape=[
            jax.ShapeDtypeStruct((2, D, MTOK), BF),
            jax.ShapeDtypeStruct((3, D, SH), F32),
            jax.ShapeDtypeStruct((1, 3, D, FF), F32),
        ],
        in_specs=[any_] * 6,
        out_specs=[any_, vm, any_],
        scratch_shapes=[
            pltpu.VMEM((2, D, MTOK), BF), pltpu.VMEM((2, D, MTOK), BF),
            pltpu.VMEM((D, SH), BF), pltpu.VMEM((D, SH), BF), pltpu.VMEM((SH, D), BF),
            pltpu.VMEM((3, D, FF), F32),
            pltpu.VMEM((FF, LW), BF),
            pltpu.VMEM((3, 128, 2 * MTOK), BF),
            pltpu.VMEM((2, D, FC), BF),
            pltpu.VMEM((3, FC, TT), BF),
            pltpu.VMEM((2, D, MTOK), F32),
            pltpu.VMEM((2, D, MTOK), BF),
            pltpu.VMEM((3, D, FF), F32),
            pltpu.VMEM((4, 2, SH, LW), BF),
            pltpu.VMEM((4, SH, LW), BF),
            pltpu.VMEM((2, 2, SH, LW), BF),
            pltpu.VMEM((2, SH, LW), BF),
            pltpu.VMEM((2, SH, LW), BF),
            pltpu.VMEM((SH, LW), BF),
            pltpu.VMEM((4, SH, LW), BF),
            dma((8,)), dma((5,)), dma((7,)), dma((3,)), dma((4,)), dma((9,)), dma((9,)), dma((6, 3)), dma((4, 3)),
        ],
        compiler_params=pltpu.CompilerParams(
            collective_id=0, has_side_effects=True, vmem_limit_bytes=60 * 1024 * 1024),
        cost_estimate=pl.CostEstimate(flops=11_000_000_000, bytes_accessed=12_000_000, transcendentals=5_000_000),
    )(x_t, dy_t, wg, wu, wd, g)


def solution(mesh):
    def local_step(x_dev, dy_dev, gate_shard, up_shard, down_shard, g_dev):
        dx_t, grad_next, grad_layer = fused(
            jnp.swapaxes(x_dev, 1, 2), jnp.swapaxes(dy_dev, 1, 2), gate_shard, up_shard, down_shard, g_dev)
        return jnp.swapaxes(dx_t, 1, 2), grad_next, grad_layer

    in_specs = (P(None, TOK_AXES, None), P(None, TOK_AXES, None), P(None, GROUP_AXES), P(None, GROUP_AXES), P(GROUP_AXES, None), P(TOK_AXES, None, None, None))
    out_specs = (P(None, TOK_AXES, None), P(None, None, GROUP_AXES), P(TOK_AXES, None, None, None))
    return jax.shard_map(local_step, mesh=mesh, in_specs=in_specs, out_specs=out_specs, check_vma=False)
```

time: 126 us -> 50.2 us (0.40)
  blocking collectives: 60.9 us -> 0 us
  Pallas kernels: 0 us -> 44.2 us
  matrix products: 33.9 us -> 0 us
  between operations: 14.2 us -> 0.66 us
  local copies, waits for them, and re-layouts: 12.5 us -> 5.22 us
  other arithmetic: 4.62 us -> 0 us
    pallas_call x0 -> x1, Pallas kernels: none -> 44.2 us  [fused(): pl.pallas_call(body, name='mlp_bwd', out_shape=[jax.ShapeDtypeStruct((2,...]
    dot_general x8 -> x0, matrix products: 33.9 us -> none  [the longest x1 11.2 us: mlp_backward(): jnp.einsum('td,fd->tf', dy_flat, w_down, preferred_element_type=jnp.float32)]
    all_gather x3 -> x0, blocking collectives: 31.5 us -> none  [the longest x1 11.5 us: local_step(): w_up = lax.all_gather(up_shard, GROUP_AXES, axis=1, tiled=True)]
    psum x1 -> x0, blocking collectives: 29.3 us -> none  [local_step(): grad_next = lax.psum(g_shard.astype(jnp.float32), 'dp')]
    reshape x3 -> x0, local copies, waits for them, and re-layouts: 4.49 us -> none  [the longest x1 1.7 us: local_step(): x_dev.reshape(micro_count * tok_dev, d_model)]
    convert_element_type x1 -> x0, other arithmetic: 2.94 us -> none  [local_step(): g_dev[0].astype(jnp.bfloat16)]
    unnamed x18 -> x7, local copies, waits for them, and re-layouts: 8.01 us -> 5.22 us
    broadcast_in_dim x1 -> x0, other arithmetic: 1.67 us -> none  [local_step(): grad_layer[None]]
  transfers between devices with their start and end apart: 1 -> 0, of which waited for: 0 -> 0; matrix products, arithmetic and copies ran while one was open for 32% -> 0% of each run, Pallas kernels for 0% -> 0%
where the time goes in v1:
time: 50.2 us; the launch traced here: 50.1 us
  Pallas kernels  44.2 us (88%)
  local copies, waits for them, and re-layouts  5.22 us (10%)
  between operations  0.66 us (1%)
    pallas_call x1, Pallas kernels, fused(): pl.pallas_call(body, name='mlp_bwd', out_shape=[jax.ShapeDtypeStruct((2,...  44.2 us
    unnamed x7, local copies, waits for them, and re-layouts  5.22 us

profile of v1, /device:TPU:0, one launch (start us, length us, event | category | flops | bytes accessed | tf_op | source)
XLA Modules:
  0.0 50.1 jit_solution(5603824354334738881)
XLA Ops:
  0.6 44.2 %mlp_bwd.1 = (bf16[2,288,1536]{2,1,0:T(8,128)(2,1)}, f32[3,288,96]{2,1,0:T(8,128)}, f32[1,3,288,768]{3,2,1,0:T(8,128)}) custom-call(bf16[2,288,1536]{2,1,0:T(8,128)(2,1)} %bitcast.4, bf16[2,288,1536]{2,1,0:T(8,128)(2,1)} %bitcast.5, bf16[288,96]{1,0:T(8,128)(2,1)} %wg_hbm.1, bf16[288,96]{1,0:T(8,128)(2,1)} %wu_hbm.1, bf16[96,288]{1,0:T(8,128)(2,1)} %wd_hbm.1, ...), custom_call_target="tpu_custom_call" | custom-call | flops 11000000512 | bytes 12000000 | tf_op jit(solution)/shard_map/mlp_bwd/pallas_call | solution.py:378
  44.8 0.0 copy-start.1
  44.8 0.0 copy-start
  44.9 2.9 %copy.12 = bf16[2,1536,288]{1,2,0:T(8,128)(2,1)} copy(bf16[2,1536,288]{1,2,0:T(8,128)(2,1)} %bitcast.3) | data formatting | bytes 3538944
  47.8 0.0 copy-done.1
  47.8 0.8 %copy.13 = f32[3,288,96]{2,1,0:T(8,128)} copy(f32[3,288,96]{2,1,0:T(8,128)S(1)} %copy-done.1) | data formatting | bytes 663552
  48.6 0.0 copy-done
  48.6 1.5 %copy.14 = f32[1,3,288,768]{3,2,1,0:T(8,128)} copy(f32[1,3,288,768]{3,2,1,0:T(8,128)S(1)} %copy-done) | data formatting | bytes 5308416
Async XLA Ops:
  44.8 3.0 %copy-start.1 = (f32[3,288,96]{2,1,0:T(8,128)S(1)}, f32[3,288,96]{2,1,0:T(8,128)}, u32[]{:S(2)}) copy-start(f32[3,288,96]{2,1,0:T(8,128)} %get-tuple-element.13) | copy-start | bytes 995332
  44.8 3.7 %copy-start = (f32[1,3,288,768]{3,2,1,0:T(8,128)S(1)}, f32[1,3,288,768]{3,2,1,0:T(8,128)}, u32[]{:S(2)}) copy-start(f32[1,3,288,768]{3,2,1,0:T(8,128)} %get-tuple-element.14) | copy-start | bytes 7962628

commit v2 on v0

v2 whole, which is shorter than its diff:
```python
import functools
import jax
import jax.numpy as jnp
from jax import lax
from jax.experimental import pallas as pl
from jax.experimental.pallas import tpu as pltpu
from jax.sharding import PartitionSpec as P

TOK_AXES = ("dp", "row", "fsdp")
GROUP_AXES = ("row", "fsdp")
MESH = pl.DeviceIdType.MESH
BF = jnp.bfloat16
F32 = jnp.float32

D = 288
FF = 768
SH = 96
LW = 896
FC = 256
TT = 256
MTOK = 1536
PIECES = ((0, 2), (2, 4), (4, 7))
NP = len(PIECES)
SUMMED = (0, 1)
NL = LW // 128
NT_DIMS = (((1,), (1,)), ((), ()))
CUTS = (
    (0, 0, 0, 0, 96), (0, 96, 1, 0, 96), (0, 192, 2, 0, 64),
    (1, 0, 2, 64, 32), (1, 32, 3, 0, 96), (1, 128, 4, 0, 96), (1, 224, 5, 0, 32),
    (2, 0, 5, 32, 64), (2, 64, 6, 0, 96), (2, 160, 7, 0, 96),
)


def dot(a, b):
    return jnp.dot(a, b, preferred_element_type=F32)


def dot_nt(a, b):
    return lax.dot_general(a, b, NT_DIMS, preferred_element_type=F32)


def eye(n):
    r = lax.broadcasted_iota(jnp.int32, (n, n), 0)
    c = lax.broadcasted_iota(jnp.int32, (n, n), 1)
    return (r == c).astype(F32).astype(BF)


PRE = ("send_p", "send_64", "send_y.0", "send_y.1", "g.0", "g.1", "g.2", "send_x.0", "send_x.1", "tails", "own_p",)
EVENTS = {
    2: ("pair.0", "pair.1", "pair.2",),
    8: ("pass64",),
    11: ("x64",),
    23: ("ph1.0", "ph1.1", "y",),
    27: ("ph1.2", "xrest",),
    30: ("ph2.0", "ph2.1", "rest2",),
    36: ("ph2.2",),
    42: ("diag", "relay.0",),
    49: ("rest3", "relay.1",),
    55: ("relay.2",),
    68: ("zall.0", "zall.1", "zall.2",),
}


def body(x_hbm, dy_hbm, wg_hbm, wu_hbm, wd_hbm, g_hbm,
         dx_ref, dw_ref, zb, tot,
         xt, yt, hh, wn, dxacc, wg, wu, wd, g32, wire, wc, xtail,
         gt, gr, s1, r1, s2, r2,
         in_sem, ws_sem, wrd_sem, wrp_sem, gs_sem, gr_sem, zs_sem, zr_sem, ts_sem, tr_sem):
    z = lax.axis_index("dp")
    y = lax.axis_index("row")
    f = lax.axis_index("fsdp")
    x = f // 2
    c = f % 2
    ny = 1 - y
    partner = (z, y, f + 1 - 2 * c)
    nbr_x = (z, y, (f + 2) % 4)
    nbr_y = (z, ny, f)
    nbr_a = (z, y + (1 - c) * (1 - 2 * y), (f + 2 * c) % 4)
    nbr_b = (z, y + c * (1 - 2 * y), (f + 2 * (1 - c)) % 4)
    ax_a = 1 - c
    ax_b = c
    split = c == 1 - x
    gets = c == x

    g_loads = [pltpu.make_async_copy(g_hbm.at[0, k], g32.at[k], in_sem.at[k]) for k in range(3)]
    w_loads = [
        pltpu.make_async_copy(wg_hbm, wg, in_sem.at[9]),
        pltpu.make_async_copy(wu_hbm, wu, in_sem.at[10]),
        pltpu.make_async_copy(wd_hbm, wd, in_sem.at[11]),
    ]
    x_loads = [
        pltpu.make_async_copy(x_hbm, xt, in_sem.at[12]),
        pltpu.make_async_copy(dy_hbm, yt, in_sem.at[13]),
    ]
    for l in w_loads + g_loads + x_loads:
        l.start()

    bar = pltpu.get_barrier_semaphore()
    for dev in (partner, nbr_a, nbr_b):
        pl.semaphore_signal(bar, inc=1, device_id=dev, device_id_type=MESH)

    mid = jnp.logical_or(z == 1, z == 2)
    end = jnp.logical_not(mid)
    near = jnp.where(z == 0, 1, jnp.where(z == 3, 2, 3 - z))
    far = jnp.where(z == 0, 2, jnp.where(z == 3, 1, jnp.where(z == 1, 3, 0)))
    mine = jnp.where(z == 1, 0, 3)

    pl.semaphore_signal(bar, inc=1, device_id=(near, y, f), device_id_type=MESH)
    pl.semaphore_signal(bar, inc=1, device_id=(far, y, f), device_id_type=MESH)

    @pl.when(mid)
    def _():
        pl.semaphore_signal(bar, inc=1, device_id=(mine, y, f), device_id_type=MESH)

    def ds(start, n):
        return pl.ds(pl.multiple_of(start, 32), n)

    def rows_of(yy, xx, cc):
        return ds((4 * yy + 2 * xx + cc) * SH, SH)

    own = rows_of(y, x, c)
    i96 = eye(SH)
    for l in w_loads:
        l.wait()
    wire[own, 0:256] = dot_nt(i96, wg[0:256, :]).astype(BF)
    wire[own, 256:512] = dot_nt(i96, wu[0:256, :]).astype(BF)
    wire[own, 512:768] = wd[:, 0:256]
    tails = dot_nt(i96, jnp.concatenate([wg[256:288, :], wu[256:288, :]], 0)).astype(BF)
    wire[own, 768:896] = jnp.concatenate([tails, wd[:, 256:288], jnp.zeros((SH, 32), BF)], 1)

    @pl.when(mid)
    def _():
        pl.semaphore_wait(bar, 6)

    @pl.when(end)
    def _():
        pl.semaphore_wait(bar, 5)

    def remote(src, dst, ssem, rsem, dev):
        return pltpu.make_async_remote_copy(src_ref=src, dst_ref=dst, send_sem=ssem, recv_sem=rsem,
                                            device_id=dev, device_id_type=MESH)

    def wcopy(rows, send, recv, dev):
        return remote(wire.at[rows], wire.at[rows], ws_sem.at[send], recv, dev)

    def wrecv(rows, sem):
        wcopy(rows, 0, sem, partner).wait_recv()

    def r64(xs):
        return ds(384 * y + 128 + 64 * xs, 64)

    def r32(xs):
        return ds(384 * y + 96 + 160 * xs, 32)

    sends = []

    def start(cp, cond=None):
        sends.append((cp, cond))
        if cond is None:
            cp.start()
        else:
            @pl.when(cond)
            def _():
                cp.start()

    def ev_send_p():
        start(wcopy(own, 1, wrp_sem.at[0], partner))

    def ev_send_64():
        start(wcopy(r64(x), 0, wrd_sem.at[0], nbr_x), split)

    def ev_send_y(core):
        start(wcopy(own, 2, wrd_sem.at[2], nbr_y), c == core)

    def ev_send_x(part):
        if part == 0:
            start(wcopy(r32(x), 3, wrd_sem.at[1], nbr_x), split)
        else:
            start(wcopy(own, 3, wrd_sem.at[1], nbr_x), jnp.logical_not(split))

    i256 = eye(256)

    def pair_copy(p):
        lo, hi = PIECES[p]
        return remote(gt.at[lo:hi, :, 1 - c], gr.at[lo:hi], gs_sem.at[p], gr_sem.at[p], partner)

    def put(o, fb, t):
        for blk, r0, sh, r, m in CUTS:
            if blk == fb:
                gt[t, sh // 2, sh % 2, r:r + m, :] = o[r0:r0 + m]

    def ready(*tiles):
        for p in range(NP):
            if PIECES[p][1] - 1 in tiles:
                start(pair_copy(p))

    def ev_g(k):
        g_loads[k].wait()
        for fb in range(3):
            o = dot_nt(i256, g32[k, 0:256, 256 * fb:256 * fb + 256].astype(BF)).astype(BF)
            put(o[:, 0:128], fb, 2 * k)
            put(o[:, 128:256], fb, 2 * k + 1)
        if k == 2:
            for fb in range(3):
                tl = jnp.concatenate([g32[j, 256:288, 256 * fb:256 * fb + 256].astype(BF) for j in range(3)]
                                     + [jnp.zeros((32, 256), BF)], 0)
                put(dot_nt(i256, tl).astype(BF), fb, 6)
        ready(*((2 * k, 2 * k + 1) if k < 2 else (4, 5, 6)))

    def ev_tails():
        for l in x_loads:
            l.wait()
        for m in range(2):
            xtl = xt[m, 256:288]
            xtail[0, m] = jnp.concatenate([xtl, jnp.zeros((96, MTOK), BF)], 0)
            xtail[1, m] = jnp.concatenate([jnp.zeros((32, MTOK), BF), xtl, jnp.zeros((64, MTOK), BF)], 0)
            xtail[2, m] = jnp.concatenate([jnp.zeros((64, MTOK), BF), yt[m, 256:288], jnp.zeros((32, MTOK), BF)], 0)

    def chip(ra, rb):
        ya_ = y + (1 - 2 * y) * (ra * ax_a + rb * ax_b)
        xa_ = x + (1 - 2 * x) * (ra * ax_b + rb * ax_a)
        return 2 * ya_ + xa_

    def add(p, q):
        return (p.astype(F32) + q.astype(F32)).astype(BF)

    def ph1(p):
        lo, hi = PIECES[p]
        return remote(s1.at[1, lo:hi], r1.at[lo:hi], gs_sem.at[NP + p], gr_sem.at[NP + p], nbr_a)

    def ph2(p):
        lo, hi = PIECES[p]
        return remote(s2.at[1, lo:hi], r2.at[lo:hi], gs_sem.at[2 * NP + p], gr_sem.at[2 * NP + p], nbr_b)

    def zcopy(slot, p, send, dev):
        lo, hi = PIECES[p]
        return remote(zb.at[slot, lo:hi], zb.at[slot, lo:hi], zs_sem.at[send, p], zr_sem.at[slot, p], (dev, y, f))

    def ev_pair(p):
        lo, hi = PIECES[p]
        pair_copy(p).wait_recv()
        for ra in (1, 0):
            for rb in range(2):
                q = chip(ra, rb)
                s1[ra, lo:hi, rb] = add(gt[lo:hi, q, c], gr[lo:hi, q])
            if ra == 1:
                start(ph1(p))

    def ev_ph1(p):
        lo, hi = PIECES[p]
        ph1(p).wait_recv()
        s2[1, lo:hi] = add(s1[0, lo:hi, 1], r1[lo:hi, 1])
        start(ph2(p))
        s2[0, lo:hi] = add(s1[0, lo:hi, 0], r1[lo:hi, 0])

    def ev_ph2(p):
        lo, hi = PIECES[p]
        ph2(p).wait_recv()
        zb[z, lo:hi] = add(s2[0, lo:hi], r2[lo:hi])
        if p in SUMMED:
            start(zcopy(z, p, 1, far), end)
            start(zcopy(z, p, 0, near))
        else:
            start(zcopy(z, p, 1, far))
            start(zcopy(z, p, 0, near))
            start(zcopy(z, p, 2, mine), mid)

    def tcopy(p):
        lo, hi = PIECES[p]
        return remote(tot.at[lo:hi], tot.at[lo:hi], ts_sem.at[p], tr_sem.at[p], (mine, y, f))

    def ev_relay(p):
        @pl.when(mid)
        def _():
            zcopy(far, p, 0, near).wait_recv()
        if p in SUMMED:
            lo, hi = PIECES[p]

            @pl.when(mid)
            def _():
                zcopy(near, p, 0, near).wait_recv()
                zcopy(mine, p, 0, near).wait_recv()
                tot[lo:hi] = z_sum(zb, lo, hi)
            start(tcopy(p), mid)
        else:
            start(zcopy(far, p, 3, mine), mid)

    def ev_zall(p):
        if p in SUMMED:
            @pl.when(end)
            def _():
                tcopy(p).wait_recv()
        else:
            zcopy(near, p, 0, near).wait_recv()

            @pl.when(mid)
            def _():
                zcopy(mine, p, 0, near).wait_recv()

            @pl.when(end)
            def _():
                zcopy(far, p, 0, near).wait_recv()
                zcopy(3 - z, p, 0, near).wait_recv()

    def ev_own_p():
        wrecv(rows_of(y, x, 1 - c), wrp_sem.at[0])

    def ev_pass64():
        @pl.when(gets)
        def _():
            wrecv(r64(1 - x), wrd_sem.at[0])
        start(wcopy(r64(1 - x), 4, wrp_sem.at[1], partner), gets)

    def ev_x64():
        @pl.when(jnp.logical_not(gets))
        def _():
            wrecv(r64(1 - x), wrp_sem.at[1])

    def ev_xrest():
        @pl.when(gets)
        def _():
            wrecv(r32(1 - x), wrd_sem.at[1])

        @pl.when(jnp.logical_not(gets))
        def _():
            wrecv(rows_of(y, 1 - x, c), wrd_sem.at[1])
        start(wcopy(r32(1 - x), 5, wrp_sem.at[2], partner), gets)
        start(wcopy(rows_of(y, 1 - x, c), 5, wrp_sem.at[2], partner), jnp.logical_not(gets))
        start(wcopy(rows_of(y, 1 - x, c), 6, wrd_sem.at[3], nbr_y), c == 1)

    def ev_y():
        wrecv(rows_of(ny, x, c), wrd_sem.at[2])
        start(wcopy(rows_of(ny, x, c), 7, wrp_sem.at[3], partner))
        start(wcopy(rows_of(ny, x, c), 6, wrd_sem.at[3], nbr_x), c == 0)

    def ev_diag():
        wrecv(rows_of(ny, 1 - x, c), wrd_sem.at[3])
        start(wcopy(rows_of(ny, 1 - x, c), 8, wrp_sem.at[4], partner))

    def ev_rest2():
        @pl.when(gets)
        def _():
            wrecv(rows_of(y, 1 - x, 1 - c), wrp_sem.at[2])

        @pl.when(jnp.logical_not(gets))
        def _():
            wrecv(r32(1 - x), wrp_sem.at[2])
        wrecv(rows_of(ny, x, 1 - c), wrp_sem.at[3])

    def ev_rest3():
        wrecv(rows_of(ny, 1 - x, 1 - c), wrp_sem.at[4])

    handlers = {
        "pair": ev_pair, "ph1": ev_ph1, "ph2": ev_ph2, "relay": ev_relay, "zall": ev_zall, "g": ev_g, "tails": ev_tails, "send_p": ev_send_p, "send_64": ev_send_64, "send_y": ev_send_y, "send_x": ev_send_x, "own_p": ev_own_p, "x64": ev_x64, "pass64": ev_pass64,
        "xrest": ev_xrest, "y": ev_y, "diag": ev_diag, "rest2": ev_rest2, "rest3": ev_rest3,
    }

    ticks = [0]

    def run(evs):
        for ev in evs:
            name, _, arg = ev.partition(".")
            with jax.named_scope(ev.replace(".", "_")):
                handlers[name](*([int(arg)] if arg else []))

    def tick():
        run(EVENTS.get(ticks[0], ()))
        ticks[0] += 1

    def forward(w, rows, h0, n):
        for m in range(2):
            for t in range(MTOK // TT):
                forward_step(w, rows, h0, n, m, slice(t * TT, t * TT + TT))
                tick()

    def forward_step(w, rows, h0, n, m, col):
        tl = w[rows, 768:896]
        xm = xt[m, 0:256, col]
        a = dot(w[rows, 0:256], xm) + dot(tl, xtail[0, m, :, col])
        b = dot(w[rows, 256:512], xm) + dot(tl, xtail[1, m, :, col])
        dh = dot(w[rows, 512:768], yt[m, 0:256, col]) + dot(tl, xtail[2, m, :, col])
        s = 1.0 / (1.0 + jnp.exp(-a))
        act = a * s
        hh[m, ds(h0, n), col] = (dh * b * (s + act * (1.0 - s))).astype(BF)
        hh[m, ds(FC + h0, n), col] = (dh * act).astype(BF)
        hh[m, ds(2 * FC + h0, n), col] = (act * b).astype(BF)

    def natural(w, rows):
        t = dot_nt(i256[:128, :128], w[rows, 768:896]).astype(BF)
        for k in range(2):
            wn[0:256, k * FC:k * FC + FC] = dot_nt(i256, w[rows, 256 * k:256 * k + 256]).astype(BF)
            wn[256:288, k * FC:k * FC + FC] = t[32 * k:32 * k + 32]

    def backward(j, lanes):
        for m in range(2):
            for n in range(2):
                col = slice(768 * n, 768 * n + 768)
                d = dot(wn[...], hh[m, 0:2 * FC, col])
                if j == 1:
                    dxacc[m, :, col] = d
                elif j == 2:
                    dxacc[m, :, col] = d + dxacc[m, :, col]
                else:
                    dx_ref[m, :, col] = (d + dxacc[m, :, col]).astype(BF)
                tick()
        for k in range(3):
            o = grad_w(k, xt, yt, hh)
            for i, l in enumerate(lanes):
                dw_ref[0, k, :, lane_tile(l)] = o[:, 128 * i:128 * i + 128]
            tick()

    run(PRE)
    forward(wire, ds(384 * y + 192 * x, 192), 64 * x, 192)
    forward(wire, r64(1 - x), 192 * (1 - x), 64)
    first = 384 * y + 128 * x
    natural(wire, ds(first, FC))
    backward(1, (first, first + 128))

    second = (384 * y + 256 - 256 * x, 384 * ny + 256 * x)
    for i, l in enumerate(second):
        wc[128 * i:128 * i + 128] = wire[ds(l, 128)]
    full = slice(0, FC)
    forward(wc, full, 0, FC)
    natural(wc, full)
    backward(2, second)

    third = 384 * ny + 128 * (1 - x)
    forward(wire, ds(third, FC), 0, FC)
    natural(wire, ds(third, FC))
    backward(3, (third, third + 128))
    assert max(EVENTS) < ticks[0]

    for cp, cond in sends:
        if cond is None:
            cp.wait_send()
        else:
            @pl.when(cond)
            def _():
                cp.wait_send()


def lane_tile(l):
    return pl.ds(pl.multiple_of(l, 128), 128)


def grad_w(k, xt, yt, hh):
    t = yt if k == 2 else xt
    hk = slice(k * FC, k * FC + FC)
    return dot_nt(t[0], hh[0, hk]) + dot_nt(t[1], hh[1, hk])


def z_sum(zb, lo, hi):
    t = zb[0, lo:hi].astype(F32) + zb[1, lo:hi].astype(F32)
    t = t + zb[2, lo:hi].astype(F32)
    return t + zb[3, lo:hi].astype(F32)


def finish(dx, dw, zb, tot, dx_hbm, gn_hbm, dw_hbm, gno, sem):
    copies = [pltpu.make_async_copy(dw.at[0, k], dw_hbm.at[0, k], sem.at[k]) for k in range(3)]
    copies += [pltpu.make_async_copy(dx.at[m], dx_hbm.at[m], sem.at[3 + m]) for m in range(2)]
    for cp in copies:
        cp.start()
    for i in range(NL):
        piece = [lo <= i < hi for lo, hi in PIECES].index(True)
        t = tot[i] if piece in SUMMED else z_sum(zb, i, i + 1)[0]
        t = jnp.concatenate([t, jnp.zeros((32, 128), F32)], 0).T[:, 0:SH]
        if i < 6:
            gno[i // 2, 128 * (i % 2):128 * (i % 2) + 128, :] = t
        else:
            for s in range(3):
                gno[s, 256:288, :] = t[32 * s:32 * s + 32]
    copies.append(pltpu.make_async_copy(gno, gn_hbm, sem.at[5]))
    copies[-1].start()
    for cp in copies:
        cp.wait()


def fused(x_t, dy_t, wg, wu, wd, g):
    hbm = pl.BlockSpec(memory_space=pltpu.HBM)
    vm = pl.BlockSpec(memory_space=pltpu.VMEM)
    dma = pltpu.SemaphoreType.DMA
    state = [pltpu.VMEM((2, D, MTOK), BF), pltpu.VMEM((1, 3, D, FF), F32), pltpu.VMEM((4, NL, SH, 128), BF), pltpu.VMEM((NL, SH, 128), F32)]
    args = [pltpu.with_memory_space_constraint(t, pltpu.HBM) for t in (x_t, dy_t, wg, wu, wd, g)]
    mid = pl.pallas_call(
        body,
        name="mlp_bwd",
        out_shape=state,
        in_specs=[hbm] * 6,
        out_specs=[vm] * 4,
        scratch_shapes=[
            pltpu.VMEM((2, D, MTOK), BF), pltpu.VMEM((2, D, MTOK), BF),
            pltpu.VMEM((2, 3 * FC, MTOK), BF),
            pltpu.VMEM((D, 2 * FC), BF),
            pltpu.VMEM((2, D, MTOK), F32),
            pltpu.VMEM((D, SH), BF), pltpu.VMEM((D, SH), BF), pltpu.VMEM((SH, D), BF),
            pltpu.VMEM((3, D, FF), F32),
            pltpu.VMEM((FF, LW), BF),
            pltpu.VMEM((FC, LW), BF),
            pltpu.VMEM((3, 2, 128, MTOK), BF),
            pltpu.VMEM((NL, 4, 2, SH, 128), BF),
            pltpu.VMEM((NL, 4, SH, 128), BF),
            pltpu.VMEM((2, NL, 2, SH, 128), BF),
            pltpu.VMEM((NL, 2, SH, 128), BF),
            pltpu.VMEM((2, NL, SH, 128), BF),
            pltpu.VMEM((NL, SH, 128), BF),
            dma((14,)), dma((9,)), dma((4,)), dma((5,)), dma((3 * NP,)), dma((3 * NP,)), dma((4, NP)), dma((4, NP)), dma((NP,)), dma((NP,)),
        ],
        compiler_params=pltpu.CompilerParams(
            collective_id=0, has_side_effects=True, vmem_limit_bytes=40 * 1024 * 1024),
        cost_estimate=pl.CostEstimate(flops=9_000_000_000, bytes_accessed=7_000_000, transcendentals=5_000_000),
    )(*args)
    mid = [pltpu.with_memory_space_constraint(t, pltpu.VMEM) for t in mid]
    return pl.pallas_call(
        finish,
        name="mlp_bwd_finish",
        out_shape=[pltpu.HBM((2, D, MTOK), BF), pltpu.HBM((3, D, SH), F32), pltpu.HBM((1, 3, D, FF), F32)],
        in_specs=[vm] * 4,
        out_specs=[hbm] * 3,
        scratch_shapes=[
            pltpu.VMEM((3, D, SH), F32), dma((6,)),
        ],
        compiler_params=pltpu.CompilerParams(vmem_limit_bytes=16 * 1024 * 1024),
        cost_estimate=pl.CostEstimate(flops=2_000_000, bytes_accessed=5_000_000, transcendentals=0),
    )(*mid)


def solution(mesh):
    def local_step(x_dev, dy_dev, gate_shard, up_shard, down_shard, g_dev):
        dx_t, grad_next, grad_layer = fused(
            jnp.swapaxes(x_dev, 1, 2), jnp.swapaxes(dy_dev, 1, 2), gate_shard, up_shard, down_shard, g_dev)
        return jnp.swapaxes(dx_t, 1, 2), grad_next, grad_layer

    in_specs = (P(None, TOK_AXES, None), P(None, TOK_AXES, None), P(None, GROUP_AXES), P(None, GROUP_AXES), P(GROUP_AXES, None), P(TOK_AXES, None, None, None))
    out_specs = (P(None, TOK_AXES, None), P(None, None, GROUP_AXES), P(TOK_AXES, None, None, None))
    return jax.shard_map(local_step, mesh=mesh, in_specs=in_specs, out_specs=out_specs, check_vma=False)
```

time: 126 us -> 34 us (0.27)
  blocking collectives: 60.9 us -> 0 us
  matrix products: 33.9 us -> 0 us
  Pallas kernels: 0 us -> 33.1 us
  between operations: 14.2 us -> 0.8 us
  local copies, waits for them, and re-layouts: 12.5 us -> 0 us
  other arithmetic: 4.62 us -> 0 us
    dot_general x8 -> x0, matrix products: 33.9 us -> none  [the longest x1 11.2 us: mlp_backward(): jnp.einsum('td,fd->tf', dy_flat, w_down, preferred_element_type=jnp.float32)]
    pallas_call x0 -> x2, Pallas kernels: none -> 33.1 us  [the longest x1 30.8 us: fused(): pl.pallas_call(body, name='mlp_bwd', out_shape=state, in_specs=[hbm] * 6,...]
    all_gather x3 -> x0, blocking collectives: 31.5 us -> none  [the longest x1 11.5 us: local_step(): w_up = lax.all_gather(up_shard, GROUP_AXES, axis=1, tiled=True)]
    psum x1 -> x0, blocking collectives: 29.3 us -> none  [local_step(): grad_next = lax.psum(g_shard.astype(jnp.float32), 'dp')]
    unnamed x18 -> x0, local copies, waits for them, and re-layouts: 8.01 us -> none
    reshape x3 -> x0, local copies, waits for them, and re-layouts: 4.49 us -> none  [the longest x1 1.7 us: local_step(): x_dev.reshape(micro_count * tok_dev, d_model)]
    convert_element_type x1 -> x0, other arithmetic: 2.94 us -> none  [local_step(): g_dev[0].astype(jnp.bfloat16)]
    broadcast_in_dim x1 -> x0, other arithmetic: 1.67 us -> none  [local_step(): grad_layer[None]]
  transfers between devices with their start and end apart: 1 -> 0, of which waited for: 0 -> 0; matrix products, arithmetic and copies ran while one was open for 32% -> 0% of each run, Pallas kernels for 0% -> 0%
where the time goes in v2:
time: 34 us; the launch traced here: 33.9 us
  Pallas kernels  33.1 us (97%)
  between operations  0.8 us (2%)
    pallas_call x1, Pallas kernels, fused(): pl.pallas_call(body, name='mlp_bwd', out_shape=state, in_specs=[hbm] * 6,...  30.8 us
    pallas_call x1, Pallas kernels, fused(): pl.pallas_call(finish, name='mlp_bwd_finish', out_shape=[pltpu.HBM((2, D,...  2.27 us

profile of v2, /device:TPU:0, one launch (start us, length us, event | category | flops | bytes accessed | tf_op | source)
XLA Modules:
  0.0 33.9 jit_solution(16454564366710771662)
XLA Ops:
  0.6 30.8 %mlp_bwd.1 = (bf16[2,288,1536]{2,1,0:T(8,128)(2,1)S(1)}, f32[1,3,288,768]{3,2,1,0:T(8,128)S(1)}, bf16[4,7,96,128]{3,2,1,0:T(8,128)(2,1)S(1)}, f32[7,96,128]{2,1,0:T(8,128)S(1)}) custom-call(bf16[2,288,1536]{2,1,0:T(8,128)(2,1)} %bitcast.3, bf16[2,288,1536]{2,1,0:T(8,128)(2,1)} %bitcast.4, bf16[288,96]{1,0:T(8,128)(2,1)} %wg_hbm.1, bf16[288,96]{1,0:T(8,128)(2,1)} %wu_hbm.1, ...), custom_call_target="tpu_custom_call" | custom-call | flops 8999999488 | bytes 7000000 | tf_op jit(solution)/shard_map/mlp_bwd/pallas_call | solution.py:484
  31.4 2.3 %mlp_bwd_finish.1 = (bf16[2,288,1536]{2,1,0:T(8,128)(2,1)}, f32[3,288,96]{2,1,0:T(8,128)}, f32[1,3,288,768]{3,2,1,0:T(8,128)}) custom-call(bf16[2,288,1536]{2,1,0:T(8,128)(2,1)S(1)} %get-tuple-element.10.dx, f32[1,3,288,768]{3,2,1,0:T(8,128)S(1)} %get-tuple-element.11.dw, bf16[4,7,96,128]{3,2,1,0:T(8,128)(2,1)S(1)} %get-tuple-element.12.zb, ...), custom_call_target="tpu_custom_call" | custom-call | flops 2000000 | bytes 5000000 | tf_op jit(solution)/shard_map/mlp_bwd_finish/pallas_call | solution.py:513

commit v3 on v2

--- a/solution.py
+++ b/solution.py
@@ -24,10 +24,10 @@
 SUMMED = (0, 1)
 NL = LW // 128
 NT_DIMS = (((1,), (1,)), ((), ()))
-CUTS = (
-    (0, 0, 0, 0, 96), (0, 96, 1, 0, 96), (0, 192, 2, 0, 64),
-    (1, 0, 2, 64, 32), (1, 32, 3, 0, 96), (1, 128, 4, 0, 96), (1, 224, 5, 0, 32),
-    (2, 0, 5, 32, 64), (2, 64, 6, 0, 96), (2, 160, 7, 0, 96),
+CUTS = tuple(
+    (b, lo - FC * b, sh, lo - SH * sh, hi - lo)
+    for b in range(FF // FC) for sh in range(FF // SH)
+    for lo, hi in [(max(FC * b, SH * sh), min(FC * b + FC, SH * sh + SH))] if lo < hi
 )
 
 
@@ -48,10 +48,10 @@
 PRE = ("send_p", "send_64", "send_y.0", "send_y.1", "g.0", "g.1", "g.2", "send_x.0", "send_x.1", "tails", "own_p",)
 EVENTS = {
     2: ("pair.0", "pair.1", "pair.2",),
-    8: ("pass64",),
+    9: ("pass64",),
     11: ("x64",),
     23: ("ph1.0", "ph1.1", "y",),
-    27: ("ph1.2", "xrest",),
+    27: ("xrest", "ph1.2",),
     30: ("ph2.0", "ph2.1", "rest2",),
     36: ("ph2.2",),
     42: ("diag", "relay.0",),

time: 34 us -> 33.9 us (level)
  no operation moved by 1% of the time
where the time goes in v3:
time: 33.9 us; the launch traced here: 33.8 us
  Pallas kernels  32.9 us (97%)
  between operations  0.8 us (2%)
    pallas_call x1, Pallas kernels, fused(): pl.pallas_call(body, name='mlp_bwd', out_shape=state, in_specs=[hbm] * 6,...  30.7 us
    pallas_call x1, Pallas kernels, fused(): pl.pallas_call(finish, name='mlp_bwd_finish', out_shape=[pltpu.HBM((2, D,...  2.27 us

profile of v3, /device:TPU:0, one launch (start us, length us, event | category | flops | bytes accessed | tf_op | source)
XLA Modules:
  0.0 33.8 jit_solution(13055476152392652084)
XLA Ops:
  0.6 30.7 %mlp_bwd.1 = (bf16[2,288,1536]{2,1,0:T(8,128)(2,1)S(1)}, f32[1,3,288,768]{3,2,1,0:T(8,128)S(1)}, bf16[4,7,96,128]{3,2,1,0:T(8,128)(2,1)S(1)}, f32[7,96,128]{2,1,0:T(8,128)S(1)}) custom-call(bf16[2,288,1536]{2,1,0:T(8,128)(2,1)} %bitcast.3, bf16[2,288,1536]{2,1,0:T(8,128)(2,1)} %bitcast.4, bf16[288,96]{1,0:T(8,128)(2,1)} %wg_hbm.1, bf16[288,96]{1,0:T(8,128)(2,1)} %wu_hbm.1, ...), custom_call_target="tpu_custom_call" | custom-call | flops 8999999488 | bytes 7000000 | tf_op jit(solution)/shard_map/mlp_bwd/pallas_call | solution.py:484
  31.3 2.3 %mlp_bwd_finish.1 = (bf16[2,288,1536]{2,1,0:T(8,128)(2,1)}, f32[3,288,96]{2,1,0:T(8,128)}, f32[1,3,288,768]{3,2,1,0:T(8,128)}) custom-call(bf16[2,288,1536]{2,1,0:T(8,128)(2,1)S(1)} %get-tuple-element.10.dx, f32[1,3,288,768]{3,2,1,0:T(8,128)S(1)} %get-tuple-element.11.dw, bf16[4,7,96,128]{3,2,1,0:T(8,128)(2,1)S(1)} %get-tuple-element.12.zb, ...), custom_call_target="tpu_custom_call" | custom-call | flops 2000000 | bytes 5000000 | tf_op jit(solution)/shard_map/mlp_bwd_finish/pallas_call | solution.py:513

commit v4 on v3

--- a/solution.py
+++ b/solution.py
@@ -376,8 +376,13 @@
     def forward_step(w, rows, h0, n, m, col):
         tl = w[rows, 768:896]
         xm = xt[m, 0:256, col]
-        a = dot(w[rows, 0:256], xm) + dot(tl, xtail[0, m, :, col])
-        b = dot(w[rows, 256:512], xm) + dot(tl, xtail[1, m, :, col])
+        if n == 64:
+            ab = dot(jnp.concatenate([w[rows, 0:256], w[rows, 256:512]], 0), xm)
+            a = ab[:n] + dot(tl, xtail[0, m, :, col])
+            b = ab[n:] + dot(tl, xtail[1, m, :, col])
+        else:
+            a = dot(w[rows, 0:256], xm) + dot(tl, xtail[0, m, :, col])
+            b = dot(w[rows, 256:512], xm) + dot(tl, xtail[1, m, :, col])
         dh = dot(w[rows, 512:768], yt[m, 0:256, col]) + dot(tl, xtail[2, m, :, col])
         s = 1.0 / (1.0 + jnp.exp(-a))
         act = a * s

time: 33.9 us -> 33.9 us (level)
  no operation moved by 1% of the time
where the time goes in v4:
time: 33.9 us; the launch traced here: 33.8 us
  Pallas kernels  33 us (97%)
  between operations  0.8 us (2%)
    pallas_call x1, Pallas kernels, fused(): pl.pallas_call(body, name='mlp_bwd', out_shape=state, in_specs=[hbm] * 6,...  30.7 us
    pallas_call x1, Pallas kernels, fused(): pl.pallas_call(finish, name='mlp_bwd_finish', out_shape=[pltpu.HBM((2, D,...  2.27 us

profile of v4, /device:TPU:0, one launch (start us, length us, event | category | flops | bytes accessed | tf_op | source)
XLA Modules:
  0.0 33.8 jit_solution(4201969847443316246)
XLA Ops:
  0.6 30.7 %mlp_bwd.1 = (bf16[2,288,1536]{2,1,0:T(8,128)(2,1)S(1)}, f32[1,3,288,768]{3,2,1,0:T(8,128)S(1)}, bf16[4,7,96,128]{3,2,1,0:T(8,128)(2,1)S(1)}, f32[7,96,128]{2,1,0:T(8,128)S(1)}) custom-call(bf16[2,288,1536]{2,1,0:T(8,128)(2,1)} %bitcast.3, bf16[2,288,1536]{2,1,0:T(8,128)(2,1)} %bitcast.4, bf16[288,96]{1,0:T(8,128)(2,1)} %wg_hbm.1, bf16[288,96]{1,0:T(8,128)(2,1)} %wu_hbm.1, ...), custom_call_target="tpu_custom_call" | custom-call | flops 8999999488 | bytes 7000000 | tf_op jit(solution)/shard_map/mlp_bwd/pallas_call | solution.py:489
  31.3 2.3 %mlp_bwd_finish.1 = (bf16[2,288,1536]{2,1,0:T(8,128)(2,1)}, f32[3,288,96]{2,1,0:T(8,128)}, f32[1,3,288,768]{3,2,1,0:T(8,128)}) custom-call(bf16[2,288,1536]{2,1,0:T(8,128)(2,1)S(1)} %get-tuple-element.10.dx, f32[1,3,288,768]{3,2,1,0:T(8,128)S(1)} %get-tuple-element.11.dw, bf16[4,7,96,128]{3,2,1,0:T(8,128)(2,1)S(1)} %get-tuple-element.12.zb, ...), custom_call_target="tpu_custom_call" | custom-call | flops 2000000 | bytes 5000000 | tf_op jit(solution)/shard_map/mlp_bwd_finish/pallas_call | solution.py:518
